TPU v7x, 32 devices: a whole 2x2x4 slice. The times are simulated.
32 devices in a mesh: replica: 8 (over y, x, core), shard: 4 (over z).
Axes of the slice: x: 2, y: 2, z: 4, core: 2. Of those that a mesh axis runs over, the one named last changes fastest.
Arguments:
- params: float32 [8, 64, 28672], P('replica', 'shard'), may hold values from -6 to 6
- first_moment: float32 [8, 64, 28672], P('replica', 'shard'), may hold values from -3 to 3
- second_moment: float32 [8, 64, 28672], P('replica', 'shard'), may hold values from 0.25 to 4
- grads: bfloat16 [4, 8, 64, 28672], P(None, 'replica', 'shard'), may hold values from -6 to 6
- push_weight: float32 [8], P('replica'), may hold values from 0.5 to 2
Outputs:
- final_weights: bfloat16 [8, 64, 28672], P('replica')
All inputs are finite; a program needn't handle non-finite values.
Results may differ from a plain program's by a relative error of at most 0.001.
Values may be sent and summed in bfloat16 or wider, within the bound.
A program may use at most 64 MiB of HBM per device.

v0:
```python
import jax
import jax.numpy as jnp
from jax import lax
from jax.sharding import PartitionSpec as P

STEPS = 4


beta_one = 0.9
beta_two = 0.95
learn_rate = 0.1
decay_rate = 0.1
epsilon = 1e-08
adam_offset = 101


def passed_along(value, axis, steps):
    count = lax.axis_size(axis)
    pairs = [(source, (source + steps) % count) for source in range(count)]
    return lax.ppermute(value, axis, pairs)


def adam_block(numer, first_moment, second_moment, gradient, weight, first_fix, second_fix):
    scale = weight[:, None, None]
    current = numer / scale
    gradient = gradient.astype(jnp.float32)
    first_moment = beta_one * first_moment + (1.0 - beta_one) * gradient
    second_moment = beta_two * second_moment + (1.0 - beta_two) * gradient * gradient
    update = first_moment / first_fix / (jnp.sqrt(second_moment / second_fix) + epsilon)
    current = current - learn_rate * (update + decay_rate * current)
    return (current * scale, first_moment, second_moment)


def per_device(params, first_moment, second_moment, grads, push_weight):
    replicas = lax.axis_size("replica")
    levels = replicas.bit_length() - 1
    weight = push_weight
    numer = params * weight[:, None, None]
    for iteration in range(STEPS):
        distance = 2 ** (iteration % levels)
        count = adam_offset + iteration
        first_fix = 1.0 - beta_one**count
        second_fix = 1.0 - beta_two**count
        gradient = grads[iteration]
        numer, first_moment, second_moment = adam_block(
            numer, first_moment, second_moment, gradient, weight, first_fix, second_fix
        )
        arrived, arrived_weight = passed_along((numer, weight), "replica", distance)
        numer = 0.5 * numer + 0.5 * arrived
        weight = 0.5 * weight + 0.5 * arrived_weight
    result = (numer / weight[:, None, None]).astype(jnp.bfloat16)
    return lax.all_gather(result, "shard", axis=1, tiled=True)


def solution(mesh):
    return jax.shard_map(
        per_device,
        mesh=mesh,
        in_specs=(
            P("replica", "shard", None),
            P("replica", "shard", None),
            P("replica", "shard", None),
            P(None, "replica", "shard", None),
            P("replica"),
        ),
        out_specs=P("replica", None, None),
        check_vma=False,
    )
```

profile of v0, /device:TPU:0, one launch (start us, length us, event | category | flops | bytes accessed | tf_op | source)
XLA Modules:
  0.0 236.3 jit_solution(4807968559331361824)
XLA Ops:
  7.2 4.6 %subtract_multiply_fusion.2 = f32[1,16,28672]{2,1,0:T(8,128)S(1)} fusion(f32[1,16,28672]{2,1,0:T(8,128)} %param.5, f32[1,16,28672]{2,1,0:T(8,128)} %param.6, f32[1,16,28672]{2,1,0:T(8,128)} %param.7, f32[]{:T(128)} %bitcast.45, bf16[4,1,16,28672]{3,2,1,0:T(8,128)(2,1)} %param.8), kind=kLoop, calls=%fused_computation.32 | loop fusion | flops 8716288 | bytes 8257540 | tf_op jit(solution)/shard_map/mul | solution.py:31
  11.8 0.5 collective-permute-start
  12.3 2.6 %collective-permute-start.1 = (f32[1]{0:T(128)}, f32[1]{0:T(128)}, u32[]{:S(2)}, u32[]{:S(2)}) collective-permute-start(f32[1]{0:T(128)} %param.9), channel_id=1, source_target_pairs={{0,4},{4,8},{8,12},{12,16},{16,20},{20,24},{24,28},{28,0},{1,5},{5... | collective-permute-start | bytes 20 | tf_op jit(solution)/shard_map/ppermute | solution.py:20
  14.9 21.3 %collective-permute-done.1 = f32[1]{0:T(128)} collective-permute-done((f32[1]{0:T(128)}, f32[1]{0:T(128)}, u32[]{:S(2)}, u32[]{:S(2)}) %collective-permute-start.1) | collective-permute-done | bytes 36 | tf_op jit(solution)/shard_map/ppermute | solution.py:20
  36.8 0.0 collective-permute-done
  36.8 2.2 subtract_multiply_fusion.1
  39.1 1.4 collective-permute-start.2
  40.5 38.5 %collective-permute-start.3 = (f32[1]{0:T(128)}, f32[1]{0:T(128)}, u32[]{:S(2)}, u32[]{:S(2)}) collective-permute-start(f32[1]{0:T(128)} %add.83), channel_id=1, source_target_pairs={{0,8},{4,12},{8,16},{12,20},{16,24},{20,28},{24,0},{28,4},{1,9},{5... | collective-permute-start | bytes 20 | tf_op jit(solution)/shard_map/ppermute | solution.py:20
  79.0 2.0 collective-permute-done.3
  81.5 0.0 collective-permute-done.2
  81.5 2.7 %subtract_multiply_fusion = f32[1,16,28672]{2,1,0:T(8,128)S(1)} fusion(f32[1,16,28672]{2,1,0:T(8,128)S(1)} %subtract_multiply_fusion.1, f32[1,16,28672]{2,1,0:T(8,128)S(1)} %collective-permute-done.2, f32[]{:T(128)} %bitcast.6, bf16[4,1,16,28672]{3,2,1,0:T(8,128)(2,1)S(1)} %copy-done.2, f32[1,16,28672]{2,1,0:T(8,128)S(1)} %copy-done, ...), kind=kLoop, calls=%fused_computation.30 | loop fusion | flops 16515072 | bytes 11927556 | tf_op jit(solution)/shard_map/mul | solution.py:31
  84.2 1.6 collective-permute-start.4
  85.8 36.7 %collective-permute-start.5 = (f32[1]{0:T(128)}, f32[1]{0:T(128)}, u32[]{:S(2)}, u32[]{:S(2)}) collective-permute-start(f32[1]{0:T(128)} %add.89), channel_id=1, source_target_pairs={{0,16},{4,20},{8,24},{12,28},{16,0},{20,4},{24,8},{28,12},{1,17},{... | collective-permute-start | bytes 20 | tf_op jit(solution)/shard_map/ppermute | solution.py:20
  122.5 1.8 collective-permute-done.5
  124.8 0.0 collective-permute-done.4
  124.9 3.1 %fusion.12 = f32[1,16,28672]{2,1,0:T(8,128)S(1)} fusion(f32[1,16,28672]{2,1,0:T(8,128)S(1)} %subtract_multiply_fusion, f32[1,16,28672]{2,1,0:T(8,128)S(1)} %collective-permute-done.4, bf16[4,1,16,28672]{3,2,1,0:T(8,128)(2,1)S(1)} %copy-done.2, f32[]{:T(128)} %bitcast.9, f32[1,16,28672]{2,1,0:T(8,128)S(1)} %copy-done, f32[1,16,28672]{2,1,0:T(8,128)S(1)} %copy-done.1), kind=kLoop, calls=%fused_computation.24 | loop fusion | flops 20185088 | bytes 12845060 | tf_op jit(solution)/shard_map/mul | solution.py:31
  128.0 0.1 collective-permute-start.6
  128.1 3.5 %collective-permute-start.7 = (f32[1]{0:T(128)}, f32[1]{0:T(128)}, u32[]{:S(2)}, u32[]{:S(2)}) collective-permute-start(f32[1]{0:T(128)} %add.95), channel_id=1, source_target_pairs={{0,4},{4,8},{8,12},{12,16},{16,20},{20,24},{24,28},{28,0},{1,5},{5... | collective-permute-start | bytes 20 | tf_op jit(solution)/shard_map/ppermute | solution.py:20
  131.6 20.1 %collective-permute-done.7 = f32[1]{0:T(128)} collective-permute-done((f32[1]{0:T(128)}, f32[1]{0:T(128)}, u32[]{:S(2)}, u32[]{:S(2)}) %collective-permute-start.7) | collective-permute-done | bytes 36 | tf_op jit(solution)/shard_map/ppermute | solution.py:20
  152.3 0.0 collective-permute-done.6
  152.3 1.2 divide_convert_fusion
  153.5 0.0 all-gather.2.cloned.1.call-update
  153.5 71.8 %all-gather.2.cloned.1.call-done = bf16[1,64,28672]{2,1,0:T(8,128)(2,1)} async-done(((bf16[1,16,28672]{2,1,0:T(8,128)(2,1)}), bf16[1,64,28672]{2,1,0:T(8,128)(2,1)}) %all-gather.2.cloned.1.call-update) | async-done | bytes 3670032 | tf_op jit(solution)/shard_map/all_gather | solution.py:52
  225.4 4.1 %copy.8 = bf16[1,64,28672]{2,1,0:T(8,128)(2,1)} copy(bf16[1,64,28672]{2,1,0:T(8,128)(2,1)} %all-gather.2.cloned.1.call-done) | data formatting | bytes 7340032
  (7 shorter events, 0.0 us)
Async XLA Ops:
  6.5 218.8 %all-gather.2.cloned.1.call-start = ((), (), s32[]{:S(2)}) async-start(), calls=%async_computation | async-start | bytes 4587520 | tf_op jit(solution)/shard_map/all_gather | solution.py:52
  7.2 29.6 %copy-start = (f32[1,16,28672]{2,1,0:T(8,128)S(1)}, f32[1,16,28672]{2,1,0:T(8,128)}, u32[]{:S(2)}) copy-start(f32[1,16,28672]{2,1,0:T(8,128)} %param.6) | copy-start | bytes 5505028
  7.2 29.6 %copy-start.1 = (f32[1,16,28672]{2,1,0:T(8,128)S(1)}, f32[1,16,28672]{2,1,0:T(8,128)}, u32[]{:S(2)}) copy-start(f32[1,16,28672]{2,1,0:T(8,128)} %param.7) | copy-start | bytes 5505028
  7.2 29.6 %copy-start.2 = (bf16[4,1,16,28672]{3,2,1,0:T(8,128)(2,1)S(1)}, bf16[4,1,16,28672]{3,2,1,0:T(8,128)(2,1)}, u32[]{:S(2)}) copy-start(bf16[4,1,16,28672]{3,2,1,0:T(8,128)(2,1)} %param.8) | copy-start | bytes 11010052
  11.8 25.0 %collective-permute-start = (f32[1,16,28672]{2,1,0:T(8,128)S(1)}, f32[1,16,28672]{2,1,0:T(8,128)S(1)}, u32[]{:S(2)}, u32[]{:S(2)}) collective-permute-start(f32[1,16,28672]{2,1,0:T(8,128)S(1)} %subtract_multiply_fusion.2), channel_id=1, source_target_pairs={{0,4},{4,8},{8,12},{12,16},{16,20},{20,24},{24,28},{28,0},{1,5},{5... | collective-permute-start | bytes 5505032 | tf_op jit(solution)/shard_map/ppermute | solution.py:20
  12.3 23.9 %collective-permute-start.1 = (f32[1]{0:T(128)}, f32[1]{0:T(128)}, u32[]{:S(2)}, u32[]{:S(2)}) collective-permute-start(f32[1]{0:T(128)} %param.9), channel_id=1, source_target_pairs={{0,4},{4,8},{8,12},{12,16},{16,20},{20,24},{24,28},{28,0},{1,5},{5... | collective-permute-start | bytes 20 | tf_op jit(solution)/shard_map/ppermute | solution.py:20
  39.1 42.5 %collective-permute-start.2 = (f32[1,16,28672]{2,1,0:T(8,128)S(1)}, f32[1,16,28672]{2,1,0:T(8,128)S(1)}, u32[]{:S(2)}, u32[]{:S(2)}) collective-permute-start(f32[1,16,28672]{2,1,0:T(8,128)S(1)} %subtract_multiply_fusion.1), channel_id=1, source_target_pairs={{0,8},{4,12},{8,16},{12,20},{16,24},{20,28},{24,0},{28,4},{1,9},{5... | collective-permute-start | bytes 5505032 | tf_op jit(solution)/shard_map/ppermute | solution.py:20
  40.5 40.5 %collective-permute-start.3 = (f32[1]{0:T(128)}, f32[1]{0:T(128)}, u32[]{:S(2)}, u32[]{:S(2)}) collective-permute-start(f32[1]{0:T(128)} %add.83), channel_id=1, source_target_pairs={{0,8},{4,12},{8,16},{12,20},{16,24},{20,28},{24,0},{28,4},{1,9},{5... | collective-permute-start | bytes 20 | tf_op jit(solution)/shard_map/ppermute | solution.py:20
  84.2 40.6 %collective-permute-start.4 = (f32[1,16,28672]{2,1,0:T(8,128)S(1)}, f32[1,16,28672]{2,1,0:T(8,128)S(1)}, u32[]{:S(2)}, u32[]{:S(2)}) collective-permute-start(f32[1,16,28672]{2,1,0:T(8,128)S(1)} %subtract_multiply_fusion), channel_id=1, source_target_pairs={{0,16},{4,20},{8,24},{12,28},{16,0},{20,4},{24,8},{28,12},{1,17},{... | collective-permute-start | bytes 5505032 | tf_op jit(solution)/shard_map/ppermute | solution.py:20
  85.8 38.5 %collective-permute-start.5 = (f32[1]{0:T(128)}, f32[1]{0:T(128)}, u32[]{:S(2)}, u32[]{:S(2)}) collective-permute-start(f32[1]{0:T(128)} %add.89), channel_id=1, source_target_pairs={{0,16},{4,20},{8,24},{12,28},{16,0},{20,4},{24,8},{28,12},{1,17},{... | collective-permute-start | bytes 20 | tf_op jit(solution)/shard_map/ppermute | solution.py:20
  128.0 24.3 %collective-permute-start.6 = (f32[1,16,28672]{2,1,0:T(8,128)S(1)}, f32[1,16,28672]{2,1,0:T(8,128)S(1)}, u32[]{:S(2)}, u32[]{:S(2)}) collective-permute-start(f32[1,16,28672]{2,1,0:T(8,128)S(1)} %fusion.12), channel_id=1, source_target_pairs={{0,4},{4,8},{8,12},{12,16},{16,20},{20,24},{24,28},{28,0},{1,5},{5... | collective-permute-start | bytes 5505032 | tf_op jit(solution)/shard_map/ppermute | solution.py:20
  128.1 23.6 %collective-permute-start.7 = (f32[1]{0:T(128)}, f32[1]{0:T(128)}, u32[]{:S(2)}, u32[]{:S(2)}) collective-permute-start(f32[1]{0:T(128)} %add.95), channel_id=1, source_target_pairs={{0,4},{4,8},{8,12},{12,16},{16,20},{20,24},{24,28},{28,0},{1,5},{5... | collective-permute-start | bytes 20 | tf_op jit(solution)/shard_map/ppermute | solution.py:20
Sparse Core Ops, SparseCore 0:
  153.7 71.6 all-gather.1
where the time goes:
time: 236 us
  waiting for transfers between devices  117 us (50%)
  starting transfers between devices  84.9 us (36%)
  between operations  16.4 us (7%)
  other arithmetic  13.8 us (6%)
  local copies, waits for them, and re-layouts  4.12 us (2%)
    ppermute x8, starting transfers between devices, passed_along(): return lax.ppermute(value, axis, pairs)  84.9 us
    all_gather x1, waiting for transfers between devices, per_device(): return lax.all_gather(result, 'shard', axis=1, tiled=True)  71.8 us
    ppermute x8, waiting for transfers between devices, passed_along(): return lax.ppermute(value, axis, pairs)  45.2 us
    mul x4, other arithmetic, adam_block(): return (current * scale, first_moment, second_moment)  12.6 us
  transfers between devices with their start and end apart: 9, of which 5 were waited for; matrix products, arithmetic and copies ran while one was open for 0% of the time, Pallas kernels for 0%

commit v1 on v0

v1 whole, which is shorter than its diff:
```python
import functools

import jax
import jax.numpy as jnp
from jax import lax
from jax.experimental import pallas as pl
from jax.experimental.pallas import tpu as pltpu
from jax.sharding import PartitionSpec as P

STEPS = 4


beta_one = 0.9
beta_two = 0.95
learn_rate = 0.1
decay_rate = 0.1
epsilon = 1e-08
adam_offset = 101

CODE_SCALE = 8.0
LAG = 2
CHUNKS = 28
MESH = pl.DeviceIdType.MESH


def plan_of(replicas):
    levels = replicas.bit_length() - 1
    distances = [2 ** (step % levels) for step in range(STEPS)]
    every = {2**level for level in range(levels)}
    plan = []
    for step, distance in enumerate(distances):
        later = set(distances[step + 1 :])
        if every <= later:
            continue
        above = {d for d in every if d > distance}
        plan.append((step, distance, above <= later))
    return plan


def encode(value):
    power = value * CODE_SCALE
    power = power * power
    power = power * power
    power = power * power
    power = power * power
    return jnp.where(value < 0.0, -power, power).astype(jnp.bfloat16)


def decode(code):
    code = code.astype(jnp.float32)
    size = jnp.exp(jnp.log(jnp.abs(code)) * (1.0 / 16.0)) * (1.0 / CODE_SCALE)
    return jnp.where(code < 0.0, -size, size)


def kernel(
    plan, replicas, shards, chunks, chunk, sub,
    params_ref, first_ref, second_ref, grads_ref, weight_ref, out_ref,
    params, first, second, grads, weights, scales, acc, terms, sent, arrived, final,
    load_sem, wsend, wrecv, xsend, xrecv, zsend, zrecv, own_sem,
):
    me, z = lax.axis_index("replica"), lax.axis_index("shard")
    rows = params.shape[0]
    rounds = len(plan)
    keep = 1.0 - learn_rate * decay_rate

    def columns(i):
        return pl.ds(pl.multiple_of(i * chunk, chunk), chunk)

    def slab(index):
        return pl.ds(pl.multiple_of(index * rows, rows), rows)

    def peer(offset):
        return lax.rem(me + offset + replicas, replicas)

    barrier = pltpu.get_barrier_semaphore()
    for k in range(1, replicas):
        pl.semaphore_signal(barrier, inc=1, device_id={"replica": peer(k)}, device_id_type=MESH)

    @pl.when(z > 0)
    def _():
        pl.semaphore_signal(barrier, inc=1, device_id={"shard": z - 1}, device_id_type=MESH)

    @pl.when(z < shards - 1)
    def _():
        pl.semaphore_signal(barrier, inc=1, device_id={"shard": z + 1}, device_id_type=MESH)

    def loads(i):
        cols = columns(i)
        return (
            pltpu.make_async_copy(params_ref.at[0, :, cols], params.at[:, cols], load_sem.at[0, i]),
            pltpu.make_async_copy(first_ref.at[0, :, cols], first.at[:, cols], load_sem.at[1, i]),
            pltpu.make_async_copy(second_ref.at[0, :, cols], second.at[:, cols], load_sem.at[2, i]),
            pltpu.make_async_copy(grads_ref.at[:, 0, :, cols], grads.at[:, :, cols], load_sem.at[3, i]),
        )

    @pl.loop(0, chunks)
    def _(i):
        for copy in loads(i):
            copy.start()

    weights[me] = jnp.full(weights.shape[1:], weight_ref[0], jnp.float32)
    ends_of_line = jnp.where(z > 0, 1, 0) + jnp.where(z < shards - 1, 1, 0)
    pl.semaphore_wait(barrier, replicas - 1 + ends_of_line)

    def weight_copy(k, owner):
        return pltpu.make_async_remote_copy(
            src_ref=weights.at[owner], dst_ref=weights.at[owner],
            send_sem=wsend.at[k - 1], recv_sem=wrecv.at[k - 1],
            device_id={"replica": peer(k)}, device_id_type=MESH,
        )

    for k in range(1, replicas):
        weight_copy(k, me).start()
    for k in range(1, replicas):
        weight_copy(k, peer(-k)).wait_recv()

    def wide(tile):
        tile = jnp.concatenate([tile] * (rows // tile.shape[0]), axis=0) if rows > tile.shape[0] else tile[:rows]
        return jnp.concatenate([tile] * (sub // tile.shape[1]), axis=1)

    levels = replicas.bit_length() - 1
    behind = [weights[peer(-k)] for k in range(replicas)]
    ends = [step for step, _, _ in plan]
    for step in range(STEPS):
        end = min(e for e in ends if e >= step)
        if step == 0:
            scales[0] = wide(behind[0] * keep ** (end + 1))
        scales[1 + step] = wide(behind[0] * (learn_rate * keep ** (end - step)))
        distance = 2 ** (step % levels)
        behind = [0.5 * behind[k] + 0.5 * behind[(k + distance) % replicas] for k in range(replicas)]
    scales[1 + STEPS] = wide(0.5 / behind[0])

    def exchange(k, i):
        _, distance, swap = plan[k]
        if swap:
            to = me + distance - 2 * distance * lax.rem(me // distance, 2)
        else:
            to = peer(distance)
        cols = columns(i)
        return pltpu.make_async_remote_copy(
            src_ref=sent.at[k, :, cols], dst_ref=arrived.at[k, :, cols],
            send_sem=xsend.at[k, i], recv_sem=xrecv.at[k, i],
            device_id={"replica": to}, device_id_type=MESH,
        )

    def gather(way, hop, i):
        sign = 1 - 2 * way
        cols, index = columns(i), z - sign * hop
        target = out_ref.at[0, slab(index), cols]
        return pltpu.make_async_remote_copy(
            src_ref=final.at[:, cols] if hop == 0 else target, dst_ref=target,
            send_sem=zsend.at[way, hop, i], recv_sem=zrecv.at[way, hop, i],
            device_id={"shard": z + sign}, device_id_type=MESH,
        )

    def gathered(way, hop, i):
        sign = 1 - 2 * way
        target = out_ref.at[0, slab(z - sign * hop), columns(i)]
        return pltpu.make_async_remote_copy(
            src_ref=target, dst_ref=target,
            send_sem=zsend.at[way, hop - 1, i], recv_sem=zrecv.at[way, hop - 1, i],
            device_id={"shard": z - sign}, device_id_type=MESH,
        )

    def has_source(way, hop):
        return z >= hop if way == 0 else z + hop < shards

    def has_target(way):
        return z < shards - 1 if way == 0 else z > 0

    def own(i):
        cols = columns(i)
        return pltpu.make_async_copy(final.at[:, cols], out_ref.at[0, slab(z), cols], own_sem.at[i])

    def start_round(i):
        for copy in loads(i):
            copy.wait()
        for j in range(chunk // sub):
            cols = pl.ds(pl.multiple_of(i * chunk + j * sub, sub), sub)
            m, v = first[:, cols], second[:, cols]
            total = scales[0] * params[:, cols]
            k = 0
            for step in range(STEPS):
                g = grads[step, :, cols].astype(jnp.float32)
                count = adam_offset + step
                m = beta_one * m + (1.0 - beta_one) * g
                v = beta_two * v + (1.0 - beta_two) * g * g
                fixed = jnp.sqrt(v * (1.0 / (1.0 - beta_two**count))) + epsilon
                update = m * (1.0 / (1.0 - beta_one**count)) / fixed * scales[1 + step]
                total = -update if total is None else total - update
                if step == ends[k]:
                    if k == 0:
                        acc[:, cols] = total
                        sent[0, :, cols] = encode(total)
                    else:
                        terms[k - 1, :, cols] = total
                    total, k = None, k + 1
        exchange(0, i).start()

    def next_round(k, i):
        exchange(k - 1, i).wait_recv()
        for j in range(chunk // sub):
            cols = pl.ds(pl.multiple_of(i * chunk + j * sub, sub), sub)
            both = acc[:, cols] + decode(arrived[k - 1, :, cols])
            if k < rounds:
                both = both * (0.5 * keep ** (ends[k] - ends[k - 1])) + terms[k - 1, :, cols]
                acc[:, cols] = both
                sent[k, :, cols] = encode(both)
            else:
                final[:, cols] = (both * scales[1 + STEPS]).astype(jnp.bfloat16)
        if k < rounds:
            exchange(k, i).start()
        else:
            for way in range(2):
                pl.when(has_target(way))(lambda way=way: gather(way, 0, i).start())
            own(i).start()

    def pass_on(hop, i):
        for way in range(2):

            @pl.when(jnp.logical_and(has_target(way), has_source(way, hop)))
            def _(way=way):
                gathered(way, hop, i).wait_recv()
                gather(way, hop, i).start()

    hops = shards - 2

    @pl.loop(0, chunks + (rounds + max(hops, 0)) * LAG)
    def _(t):
        def at(stage, act):
            i = t - stage * LAG

            @pl.when(jnp.logical_and(i >= 0, i < chunks))
            def _():
                act(i)

        at(0, start_round)
        for k in range(1, rounds + 1):
            at(k, functools.partial(next_round, k))
        for hop in range(1, hops + 1):
            at(rounds + hop, functools.partial(pass_on, hop))

    for k in range(1, replicas):
        weight_copy(k, me).wait_send()

    @pl.loop(0, chunks)
    def _(i):
        for k in range(rounds):
            exchange(k, i).wait_send()
        own(i).wait()
        for way in range(2):
            for hop in range(shards - 1):

                @pl.when(jnp.logical_and(has_target(way), has_source(way, hop)))
                def _(way=way, hop=hop):
                    gather(way, hop, i).wait_send()

            for hop in range(1, shards):
                unread = jnp.logical_not(has_target(way))

                @pl.when(jnp.logical_and(unread, has_source(way, hop)))
                def _(way=way, hop=hop):
                    gathered(way, hop, i).wait_recv()


def per_device(params, first_moment, second_moment, grads, push_weight):
    replicas, shards = lax.axis_size("replica"), lax.axis_size("shard")
    _, rows, cols = params.shape
    units = cols // 128
    chunks = max(n for n in range(1, CHUNKS + 1) if units % n == 0)
    chunk = cols // chunks
    sub = max(128 * n for n in (1, 2) if chunk % (128 * n) == 0)
    plan = plan_of(replicas)
    rounds = len(plan)
    f32, bf16, dma = jnp.float32, jnp.bfloat16, pltpu.SemaphoreType.DMA
    anywhere = pl.BlockSpec(memory_space=pl.ANY)
    body = functools.partial(kernel, plan, replicas, shards, chunks, chunk, sub)
    hops = max(shards - 1, 1)
    return pl.pallas_call(
        body,
        out_shape=jax.ShapeDtypeStruct((1, rows * shards, cols), bf16),
        in_specs=[anywhere] * 4 + [pl.BlockSpec(memory_space=pltpu.SMEM)],
        out_specs=anywhere,
        scratch_shapes=[
            pltpu.VMEM((rows, cols), f32),
            pltpu.VMEM((rows, cols), f32),
            pltpu.VMEM((rows, cols), f32),
            pltpu.VMEM((STEPS, rows, cols), bf16),
            pltpu.VMEM((replicas, 8, 128), f32),
            pltpu.VMEM((STEPS + 2, rows, sub), f32),
            pltpu.VMEM((rows, cols), f32),
            pltpu.VMEM((max(rounds - 1, 1), rows, cols), f32),
            pltpu.VMEM((rounds, rows, cols), bf16),
            pltpu.VMEM((rounds, rows, cols), bf16),
            pltpu.VMEM((rows, cols), bf16),
            dma((4, chunks)),
            dma((replicas - 1,)),
            dma((replicas - 1,)),
            dma((rounds, chunks)),
            dma((rounds, chunks)),
            dma((2, hops, chunks)),
            dma((2, hops, chunks)),
            dma((chunks,)),
        ],
        compiler_params=pltpu.CompilerParams(
            collective_id=0, has_side_effects=True, vmem_limit_bytes=60 * 1024 * 1024
        ),
    )(params, first_moment, second_moment, grads, push_weight)


def solution(mesh):
    return jax.shard_map(
        per_device,
        mesh=mesh,
        in_specs=(
            P("replica", "shard", None),
            P("replica", "shard", None),
            P("replica", "shard", None),
            P(None, "replica", "shard", None),
            P("replica"),
        ),
        out_specs=P("replica", None, None),
        check_vma=False,
    )
```

time: 236 us -> 89.3 us (0.38)
  waiting for transfers between devices: 117 us -> 0 us
  starting transfers between devices: 84.9 us -> 0 us
  Pallas kernels: 0 us -> 84.3 us
  between operations: 16.4 us -> 0.66 us
  other arithmetic: 13.8 us -> 0 us
    ppermute x8 -> x0, starting transfers between devices: 84.9 us -> none  [passed_along(): return lax.ppermute(value, axis, pairs)]
    pallas_call x0 -> x1, Pallas kernels: none -> 84.3 us  [per_device(): pl.pallas_call(body, out_shape=jax.ShapeDtypeStruct((1, rows * shards, co...]
    all_gather x1 -> x0, waiting for transfers between devices: 71.8 us -> none  [per_device(): return lax.all_gather(result, 'shard', axis=1, tiled=True)]
    ppermute x8 -> x0, waiting for transfers between devices: 45.2 us -> none  [passed_along(): return lax.ppermute(value, axis, pairs)]
    mul x4 -> x0, other arithmetic: 12.6 us -> none  [adam_block(): return (current * scale, first_moment, second_moment)]
  transfers between devices with their start and end apart: 9 -> 0, of which waited for: 5 -> 0; matrix products, arithmetic and copies ran while one was open for 0% -> 0% of each run, Pallas kernels for 0% -> 0%
where the time goes in v1:
time: 89.3 us; the launch traced here: 89.1 us
  Pallas kernels  84.3 us (94%)
  local copies, waits for them, and re-layouts  4.11 us (5%)
    pallas_call x1, Pallas kernels, per_device(): pl.pallas_call(body, out_shape=jax.ShapeDtypeStruct((1, rows * shards, co...  84.3 us
    unnamed x1, local copies, waits for them, and re-layouts  4.11 us

profile of v1, /device:TPU:0, one launch (start us, length us, event | category | flops | bytes accessed | tf_op | source)
XLA Modules:
  0.0 89.1 jit_solution(6053479898086875770)
XLA Ops:
  0.7 84.3 %shard_map.55 = bf16[1,64,28672]{2,1,0:T(8,128)(2,1)} custom-call(f32[1,16,28672]{2,1,0:T(8,128)} %params_ref.1, f32[1,16,28672]{2,1,0:T(8,128)} %first_ref.1, f32[1,16,28672]{2,1,0:T(8,128)} %second_ref.1, bf16[4,1,16,28672]{3,2,1,0:T(8,128)(2,1)} %grads_ref.1, f32[1]{0:T(128)S(6)} %copy.7.weight_ref), custom_call_target="tpu_custom_call" | custom-call | tf_op jit(solution)/shard_map/pallas_call | solution.py:279
  85.0 4.1 %copy.8 = bf16[1,64,28672]{2,1,0:T(8,128)(2,1)} copy(bf16[1,64,28672]{2,1,0:T(8,128)(2,1)} %shard_map.55) | data formatting | bytes 7340032

commit v2 on v1

--- a/solution.py
+++ b/solution.py
@@ -19,7 +19,10 @@
 
 CODE_SCALE = 8.0
 LAG = 2
+HOP_LAG = 2
 CHUNKS = 28
+LOAD_GROUP = 4
+GATHER_GROUP = 1
 MESH = pl.DeviceIdType.MESH
 
 
@@ -53,7 +56,7 @@
 
 
 def kernel(
-    plan, replicas, shards, chunks, chunk, sub,
+    plan, replicas, shards, chunks, chunk, sub, load_group, gather_group,
     params_ref, first_ref, second_ref, grads_ref, weight_ref, out_ref,
     params, first, second, grads, weights, scales, acc, terms, sent, arrived, final,
     load_sem, wsend, wrecv, xsend, xrecv, zsend, zrecv, own_sem,
@@ -63,8 +66,8 @@
     rounds = len(plan)
     keep = 1.0 - learn_rate * decay_rate
 
-    def columns(i):
-        return pl.ds(pl.multiple_of(i * chunk, chunk), chunk)
+    def columns(i, group=1):
+        return pl.ds(pl.multiple_of(i * (group * chunk), chunk), group * chunk)
 
     def slab(index):
         return pl.ds(pl.multiple_of(index * rows, rows), rows)
@@ -85,7 +88,7 @@
         pl.semaphore_signal(barrier, inc=1, device_id={"shard": z + 1}, device_id_type=MESH)
 
     def loads(i):
-        cols = columns(i)
+        cols = columns(i, load_group)
         return (
             pltpu.make_async_copy(params_ref.at[0, :, cols], params.at[:, cols], load_sem.at[0, i]),
             pltpu.make_async_copy(first_ref.at[0, :, cols], first.at[:, cols], load_sem.at[1, i]),
@@ -93,7 +96,7 @@
             pltpu.make_async_copy(grads_ref.at[:, 0, :, cols], grads.at[:, :, cols], load_sem.at[3, i]),
         )
 
-    @pl.loop(0, chunks)
+    @pl.loop(0, chunks // load_group)
     def _(i):
         for copy in loads(i):
             copy.start()
@@ -136,29 +139,29 @@
             to = me + distance - 2 * distance * lax.rem(me // distance, 2)
         else:
             to = peer(distance)
-        cols = columns(i)
+        cols = slice(None) if i is None else columns(i)
         return pltpu.make_async_remote_copy(
             src_ref=sent.at[k, :, cols], dst_ref=arrived.at[k, :, cols],
-            send_sem=xsend.at[k, i], recv_sem=xrecv.at[k, i],
+            send_sem=xsend.at[k], recv_sem=xrecv.at[k, 0 if i is None else i],
             device_id={"replica": to}, device_id_type=MESH,
         )
 
     def gather(way, hop, i):
         sign = 1 - 2 * way
-        cols, index = columns(i), z - sign * hop
+        cols, index = slice(None) if i is None else columns(i, gather_group), z - sign * hop
         target = out_ref.at[0, slab(index), cols]
         return pltpu.make_async_remote_copy(
             src_ref=final.at[:, cols] if hop == 0 else target, dst_ref=target,
-            send_sem=zsend.at[way, hop, i], recv_sem=zrecv.at[way, hop, i],
+            send_sem=zsend.at[way, hop], recv_sem=zrecv.at[way, hop, 0 if i is None else i],
             device_id={"shard": z + sign}, device_id_type=MESH,
         )
 
     def gathered(way, hop, i):
         sign = 1 - 2 * way
-        target = out_ref.at[0, slab(z - sign * hop), columns(i)]
+        target = out_ref.at[0, slab(z - sign * hop), columns(i, gather_group)]
         return pltpu.make_async_remote_copy(
             src_ref=target, dst_ref=target,
-            send_sem=zsend.at[way, hop - 1, i], recv_sem=zrecv.at[way, hop - 1, i],
+            send_sem=zsend.at[way, hop - 1], recv_sem=zrecv.at[way, hop - 1, i],
             device_id={"shard": z - sign}, device_id_type=MESH,
         )
 
@@ -169,12 +172,15 @@
         return z < shards - 1 if way == 0 else z > 0
 
     def own(i):
-        cols = columns(i)
-        return pltpu.make_async_copy(final.at[:, cols], out_ref.at[0, slab(z), cols], own_sem.at[i])
+        cols = slice(None) if i is None else columns(i, gather_group)
+        return pltpu.make_async_copy(final.at[:, cols], out_ref.at[0, slab(z), cols], own_sem)
 
     def start_round(i):
-        for copy in loads(i):
-            copy.wait()
+        @pl.when(lax.rem(i, load_group) == 0)
+        def _():
+            for copy in loads(i // load_group):
+                copy.wait()
+
         for j in range(chunk // sub):
             cols = pl.ds(pl.multiple_of(i * chunk + j * sub, sub), sub)
             m, v = first[:, cols], second[:, cols]
@@ -211,24 +217,29 @@
         if k < rounds:
             exchange(k, i).start()
         else:
-            for way in range(2):
-                pl.when(has_target(way))(lambda way=way: gather(way, 0, i).start())
-            own(i).start()
+
+            @pl.when(lax.rem(i, gather_group) == gather_group - 1)
+            def _():
+                for way in range(2):
+                    pl.when(has_target(way))(lambda way=way: gather(way, 0, i // gather_group).start())
+                own(i // gather_group).start()
 
     def pass_on(hop, i):
         for way in range(2):
 
-            @pl.when(jnp.logical_and(has_target(way), has_source(way, hop)))
+            whole = lax.rem(i, gather_group) == gather_group - 1
+
+            @pl.when(jnp.logical_and(whole, jnp.logical_and(has_target(way), has_source(way, hop))))
             def _(way=way):
-                gathered(way, hop, i).wait_recv()
-                gather(way, hop, i).start()
+                gathered(way, hop, i // gather_group).wait_recv()
+                gather(way, hop, i // gather_group).start()
 
     hops = shards - 2
 
-    @pl.loop(0, chunks + (rounds + max(hops, 0)) * LAG)
+    @pl.loop(0, chunks + rounds * LAG + max(hops, 0) * HOP_LAG)
     def _(t):
-        def at(stage, act):
-            i = t - stage * LAG
+        def at(delay, act):
+            i = t - delay
 
             @pl.when(jnp.logical_and(i >= 0, i < chunks))
             def _():
@@ -236,31 +247,30 @@
 
         at(0, start_round)
         for k in range(1, rounds + 1):
-            at(k, functools.partial(next_round, k))
+            at(k * LAG, functools.partial(next_round, k))
         for hop in range(1, hops + 1):
-            at(rounds + hop, functools.partial(pass_on, hop))
+            at(rounds * LAG + hop * HOP_LAG, functools.partial(pass_on, hop))
+
+    for way in range(2):
+
+        @pl.when(jnp.logical_not(has_target(way)))
+        def _(way=way):
+            @pl.loop(0, chunks // gather_group)
+            def _(i):
+                for hop in range(1, shards):
+                    pl.when(has_source(way, hop))(lambda hop=hop: gathered(way, hop, i).wait_recv())
 
     for k in range(1, replicas):
         weight_copy(k, me).wait_send()
-
-    @pl.loop(0, chunks)
-    def _(i):
-        for k in range(rounds):
-            exchange(k, i).wait_send()
-        own(i).wait()
-        for way in range(2):
-            for hop in range(shards - 1):
-
-                @pl.when(jnp.logical_and(has_target(way), has_source(way, hop)))
-                def _(way=way, hop=hop):
-                    gather(way, hop, i).wait_send()
-
-            for hop in range(1, shards):
-                unread = jnp.logical_not(has_target(way))
-
-                @pl.when(jnp.logical_and(unread, has_source(way, hop)))
-                def _(way=way, hop=hop):
-                    gathered(way, hop, i).wait_recv()
+    for k in range(rounds):
+        exchange(k, None).wait_send()
+    own(None).wait()
+    for way in range(2):
+        for hop in range(shards - 1):
+
+            @pl.when(jnp.logical_and(has_target(way), has_source(way, hop)))
+            def _(way=way, hop=hop):
+                gather(way, hop, None).wait_send()
 
 
 def per_device(params, first_moment, second_moment, grads, push_weight):
@@ -270,12 +280,16 @@
     chunks = max(n for n in range(1, CHUNKS + 1) if units % n == 0)
     chunk = cols // chunks
     sub = max(128 * n for n in (1, 2) if chunk % (128 * n) == 0)
+    load_group = LOAD_GROUP if chunks % LOAD_GROUP == 0 else 1
+    gather_group = GATHER_GROUP if chunks % GATHER_GROUP == 0 else 1
     plan = plan_of(replicas)
     rounds = len(plan)
     f32, bf16, dma = jnp.float32, jnp.bfloat16, pltpu.SemaphoreType.DMA
     anywhere = pl.BlockSpec(memory_space=pl.ANY)
-    body = functools.partial(kernel, plan, replicas, shards, chunks, chunk, sub)
+    body = functools.partial(kernel, plan, replicas, shards, chunks, chunk, sub, load_group, gather_group)
     hops = max(shards - 1, 1)
+    large = (params, first_moment, second_moment, grads)
+    large = tuple(pltpu.with_memory_space_constraint(x, pltpu.HBM) for x in large)
     return pl.pallas_call(
         body,
         out_shape=jax.ShapeDtypeStruct((1, rows * shards, cols), bf16),
@@ -293,19 +307,19 @@
             pltpu.VMEM((rounds, rows, cols), bf16),
             pltpu.VMEM((rounds, rows, cols), bf16),
             pltpu.VMEM((rows, cols), bf16),
-            dma((4, chunks)),
+            dma((4, chunks // load_group)),
             dma((replicas - 1,)),
             dma((replicas - 1,)),
+            dma((rounds,)),
             dma((rounds, chunks)),
-            dma((rounds, chunks)),
-            dma((2, hops, chunks)),
-            dma((2, hops, chunks)),
-            dma((chunks,)),
+            dma((2, hops)),
+            dma((2, hops, chunks // gather_group)),
+            dma,
         ],
         compiler_params=pltpu.CompilerParams(
-            collective_id=0, has_side_effects=True, vmem_limit_bytes=60 * 1024 * 1024
+            collective_id=0, has_side_effects=True, vmem_limit_bytes=48 * 1024 * 1024
         ),
-    )(params, first_moment, second_moment, grads, push_weight)
+    )(*large, push_weight)
 
 
 def solution(mesh):

time: 89.3 us -> 83.8 us (0.938)
  Pallas kernels: 84.3 us -> 81.1 us
  local copies, waits for them, and re-layouts: 4.11 us -> 1.84 us
    pallas_call x1, Pallas kernels: 84.3 us -> 81.1 us  [per_device(): pl.pallas_call(body, out_shape=jax.ShapeDtypeStruct((1, rows * shards, co...]
    unnamed x1, local copies, waits for them, and re-layouts: 4.11 us -> 1.84 us
where the time goes in v2:
time: 83.8 us; the launch traced here: 83.6 us
  Pallas kernels  81.1 us (97%)
  local copies, waits for them, and re-layouts  1.84 us (2%)
    pallas_call x1, Pallas kernels, per_device(): pl.pallas_call(body, out_shape=jax.ShapeDtypeStruct((1, rows * shards, co...  81.1 us
    unnamed x1, local copies, waits for them, and re-layouts  1.84 us

profile of v2, /device:TPU:0, one launch (start us, length us, event | category | flops | bytes accessed | tf_op | source)
XLA Modules:
  0.0 83.6 jit_solution(16417286641781498905)
XLA Ops:
  0.7 81.1 %shard_map.55 = bf16[1,64,28672]{2,1,0:T(8,128)(2,1)S(1)} custom-call(f32[1,16,28672]{2,1,0:T(8,128)} %params_ref.1, f32[1,16,28672]{2,1,0:T(8,128)} %first_ref.1, f32[1,16,28672]{2,1,0:T(8,128)} %second_ref.1, bf16[4,1,16,28672]{3,2,1,0:T(8,128)(2,1)} %grads_ref.1, f32[1]{0:T(128)S(6)} %copy.7.weight_ref), custom_call_target="tpu_custom_call" | custom-call | tf_op jit(solution)/shard_map/pallas_call | solution.py:293
  81.8 1.8 %copy.8 = bf16[1,64,28672]{2,1,0:T(8,128)(2,1)} copy(bf16[1,64,28672]{2,1,0:T(8,128)(2,1)S(1)} %shard_map.55) | data formatting | bytes 7340032

commit v3 on v2

--- a/solution.py
+++ b/solution.py
@@ -18,10 +18,10 @@
 adam_offset = 101
 
 CODE_SCALE = 8.0
-LAG = 2
-HOP_LAG = 2
+LAG = 3
+HOP_LAG = 3
 CHUNKS = 28
-LOAD_GROUP = 4
+LOAD_GROUP = 2
 GATHER_GROUP = 1
 MESH = pl.DeviceIdType.MESH
 

time: 83.8 us -> 83.9 us (level)
  no operation moved by 1% of the time
where the time goes in v3:
time: 83.9 us; the launch traced here: 83.7 us
  Pallas kernels  81.2 us (97%)
  local copies, waits for them, and re-layouts  1.84 us (2%)
    pallas_call x1, Pallas kernels, per_device(): pl.pallas_call(body, out_shape=jax.ShapeDtypeStruct((1, rows * shards, co...  81.2 us
    unnamed x1, local copies, waits for them, and re-layouts  1.84 us

profile of v3, /device:TPU:0, one launch (start us, length us, event | category | flops | bytes accessed | tf_op | source)
XLA Modules:
  0.0 83.7 jit_solution(6726592390210896537)
XLA Ops:
  0.7 81.2 %shard_map.55 = bf16[1,64,28672]{2,1,0:T(8,128)(2,1)S(1)} custom-call(f32[1,16,28672]{2,1,0:T(8,128)} %params_ref.1, f32[1,16,28672]{2,1,0:T(8,128)} %first_ref.1, f32[1,16,28672]{2,1,0:T(8,128)} %second_ref.1, bf16[4,1,16,28672]{3,2,1,0:T(8,128)(2,1)} %grads_ref.1, f32[1]{0:T(128)S(6)} %copy.7.weight_ref), custom_call_target="tpu_custom_call" | custom-call | tf_op jit(solution)/shard_map/pallas_call | solution.py:293
  81.9 1.8 %copy.8 = bf16[1,64,28672]{2,1,0:T(8,128)(2,1)} copy(bf16[1,64,28672]{2,1,0:T(8,128)(2,1)S(1)} %shard_map.55) | data formatting | bytes 7340032
